TPU v7x, 128 devices: a whole 4x4x4 slice. The times are simulated.
128 devices in a mesh: res: 32 (over z, x, core), grp: 4 (over y).
Axes of the slice: x: 4, y: 4, z: 4, core: 2. Of those that a mesh axis runs over, the one named last changes fastest.
Arguments:
- right_side: float32 [3, 64, 64, 512], P(None, 'res', 'grp'), may hold values from -30 to 30
- accumulation: float32 [3, 3, 64, 64, 512], P(None, None, 'res', 'grp'), may hold values from -1 to 2, as said below
- transmissibility: float32 [6, 3, 3, 64, 64, 512], P(None, None, None, 'res', 'grp'), may hold values from -1 to 2, as said below
- completion: int32 [1024, 256], P(('res', 'grp')), may hold values from 0 to 16383, as said below
- live_count: int32 [1024], P(('res', 'grp')), may hold values from 64 to 256
- owner: int32 [1024, 1], P(('res', 'grp')), may hold values from 0 to 3; in each aligned block of 8 rows (0 to 7, 8 to 15, ...) at most 4 rows name the same one
- cell_to_well: float32 [1024, 3, 256], P(('res', 'grp')), may hold values from -3 to 3
- well_to_cell: float32 [1024, 3, 256], P(('res', 'grp')), may hold values from -3 to 3
- inverse: float32 [128, 4, 4, 256, 256], P(('res', 'grp')), may hold values from -1 to 2
Outputs:
- solution: float32 [3, 64, 64, 512], P(None, 'res', 'grp')
- residual: float32 [3, 64, 64, 512], P(None, 'res', 'grp')
Inputs may be any that keep to these rules, and one draw needn't show every extreme that they name: `completion`: cells may repeat. Among the 8 wells of one device at most 4 name the same owner. `accumulation`: diagonal entries positive. `transmissibility`: diagonal entries positive.
All inputs are finite; a program needn't handle non-finite values.
Results may differ from a plain program's by a relative error of at most 0.0003.
Values sent between devices are 32-bit elements; how exact they have to be, the bound alone decides.
A program may use at most 128 MiB of HBM per device.

v0:
```python
import jax
import jax.numpy as jnp
from jax import lax
from jax.sharding import Mesh
from jax.sharding import PartitionSpec as P

ITERS = 3
RES_GRP = ("res_0", "res_1", "res_2", "grp")
RES = ("res_0", "res_1", "res_2")


def extended(shard, sides, width):
    edges = {}
    for axis, dim in sides:
        devices, length = (lax.axis_size(axis), shard.shape[dim])
        up = [(i, (i + 1) % devices) for i in range(devices - 1)]
        last = lax.slice_in_dim(shard, length - width, length, axis=dim)
        leading = lax.slice_in_dim(shard, 0, width, axis=dim)
        edges[dim] = (
            lax.ppermute(last, axis, up),
            lax.ppermute(leading, axis, [(b, a) for a, b in up]),
        )
    done = []
    for _, dim in sides:
        low, high = edges[dim]
        around = [(width, width) if d in done else (0, 0) for d in range(shard.ndim)]
        shard = jnp.concatenate([jnp.pad(low, around), shard, jnp.pad(high, around)], axis=dim)
        done.append(dim)
    return shard


def over_axes(shard, axes):
    for axis in axes:
        shard = lax.psum(shard, axis)
    return shard


def neighbours(vector):
    padded = extended(vector, ((RES, 1), ("grp", 2)), 1)
    zpadded = jnp.pad(vector, ((0, 0), (0, 0), (0, 0), (1, 1)))
    return [
        padded[:, 2:, 1:-1, :],
        padded[:, :-2, 1:-1, :],
        padded[:, 1:-1, 2:, :],
        padded[:, 1:-1, :-2, :],
        zpadded[..., 2:],
        zpadded[..., :-2],
    ]


def stencil(vector, diag_total, transmissibility):
    beside_list = neighbours(vector)
    result = jnp.sum(diag_total * vector[None], axis=1)
    for face in range(6):
        result = result - jnp.sum(transmissibility[face] * beside_list[face][None], axis=1)
    return result


def body(
    right_side,
    accumulation,
    transmissibility,
    completion,
    live_count,
    owner,
    cell_to_well,
    well_to_cell,
    inverse,
):
    highest = lax.Precision.HIGHEST
    components, cells_x, cells_y, cells_z = right_side.shape
    blocks, segb = completion.shape
    capacity = inverse.shape[2]
    groups = lax.axis_size("grp")
    flat_index = completion.reshape(-1)
    open_mask = (jnp.arange(segb, dtype=jnp.int32)[None, :] < live_count[:, None]).astype(
        jnp.float32
    )
    owner_eq = (owner == jnp.arange(groups, dtype=jnp.int32)[None, :]).astype(jnp.int32)
    prior = jnp.cumsum(owner_eq, axis=0) - owner_eq
    slot_number = jnp.sum(prior * owner_eq, axis=1)
    target = owner[:, 0] * capacity + slot_number
    packing = (target[:, None] == jnp.arange(groups * capacity, dtype=jnp.int32)[None, :]).astype(
        jnp.float32
    )
    diag_total = accumulation
    for face in range(6):
        diag_total = diag_total + transmissibility[face]
    moved = lax.all_to_all(inverse[0], "grp", split_axis=0, concat_axis=0, tiled=True)
    block_inverse = jnp.einsum(
        "bq,qst->bst", packing, moved.reshape(groups * capacity, segb, segb), precision=highest
    )

    def solve_wells(coupled):
        return jnp.einsum("bst,bt->bs", block_inverse, coupled, precision=highest)

    def operator(vector):
        result = stencil(vector, diag_total, transmissibility)
        flat = vector.reshape(components, -1)
        picked = jnp.moveaxis(flat[:, flat_index].reshape(components, blocks, segb), 0, 1)
        coupled = jnp.sum(cell_to_well * picked, axis=1) * open_mask
        well_value = solve_wells(coupled)
        correction = well_to_cell * (well_value * open_mask)[:, None, :]
        correction = jnp.moveaxis(correction, 0, 1).reshape(components, -1)
        out_flat = result.reshape(components, -1).at[:, flat_index].add(-correction)
        return out_flat.reshape(vector.shape)

    solution = jnp.zeros_like(right_side)
    residual = right_side
    search = right_side
    rho = over_axes(jnp.sum(residual * residual), RES_GRP)
    for index in range(ITERS):
        image = operator(search)
        alpha = rho / over_axes(jnp.sum(right_side * image), RES_GRP)
        middle = residual - alpha * image
        second = operator(middle)
        inner, square, along_middle, along_second = (
            over_axes(jnp.sum(second * middle), RES_GRP),
            over_axes(jnp.sum(second * second), RES_GRP),
            over_axes(jnp.sum(right_side * middle), RES_GRP),
            over_axes(jnp.sum(right_side * second), RES_GRP),
        )
        omega = inner / square
        solution = solution + alpha * search + omega * middle
        residual = middle - omega * second
        rho_next = along_middle - omega * along_second
        if index + 1 < ITERS:
            search = residual + rho_next / rho * (alpha / omega) * (search - omega * image)
            rho = rho_next
    return (solution, residual)


def solution(mesh):
    finer = Mesh(
        mesh.devices.reshape(4, 4, 2, mesh.shape["grp"]), ("res_0", "res_1", "res_2", "grp")
    )
    in_specs = (
        P(None, RES, "grp", None),
        P(None, None, RES, "grp", None),
        P(None, None, None, RES, "grp", None),
        P(RES_GRP, None),
        P(RES_GRP),
        P(RES_GRP, None),
        P(RES_GRP, None, None),
        P(RES_GRP, None, None),
        P(RES_GRP, None, None, None, None),
    )
    out_specs = (P(None, RES, "grp", None), P(None, RES, "grp", None))
    return jax.shard_map(body, mesh=finer, in_specs=in_specs, out_specs=out_specs, check_vma=False)
```

profile of v0, /device:TPU:10, one launch (start us, length us, event | category | flops | bytes accessed | tf_op | source)
XLA Modules:
  0.0 719.2 jit_solution(10837892056741657385)
XLA Ops:
  27.1 11.0 %gather_fusion = f32[2048,3]{1,0:T(8,128)} fusion(f32[3,16384]{0,1:T(8,128)} %bitcast.284, s32[2048]{0:T(1024)S(1)} %broadcast_clamp_fusion), kind=kCustom, calls=%fused_computation | custom fusion | bytes 57344 | tf_op jit(solution)/shard_map/gather | solution.py:100
  74.2 17.4 %scatter_fusion = f32[3,16384]{0,1:T(8,128)} fusion(f32[3,16384]{0,1:T(8,128)} %bitcast.273, s32[2048]{0:T(1024)S(1)} %bitcast.299, f32[2048,3]{1,0:T(8,128)} %bitcast.291), kind=kCustom, calls=%fused_computation.6 | custom fusion | flops 6144 | bytes 81920 | tf_op jit(solution)/shard_map/scatter-add | solution.py:105
  99.1 12.4 %all-reduce.29 = (f32[]{:T(128)}, f32[]{:T(128)}) all-reduce(f32[]{:T(128)} %get-tuple-element.45, f32[]{:T(128)} %get-tuple-element.44), channel_id=1, replica_groups=mesh['res_0'=4,'res_1'=4,'res_2'=2,'grp'=4] {'res_0'}, use_global_device_ids=true, to_apply=%region_1.2 | all-reduce | flops 2 | bytes 16 | tf_op jit(solution)/shard_map/psum | solution.py:34
  111.6 11.0 %all-reduce.25 = (f32[]{:T(128)}, f32[]{:T(128)}) all-reduce(f32[]{:T(128)} %get-tuple-element.80, f32[]{:T(128)} %get-tuple-element.81), channel_id=1, replica_groups=mesh['res_0'=4,'res_1'=4,'res_2'=2,'grp'=4] {'res_1'}, use_global_device_ids=true, to_apply=%region_2.3 | all-reduce | flops 2 | bytes 16 | tf_op jit(solution)/shard_map/psum | solution.py:34
  125.8 8.7 %all-reduce.21 = (f32[]{:T(128)}, f32[]{:T(128)}) all-reduce(f32[]{:T(128)} %get-tuple-element.92, f32[]{:T(128)} %get-tuple-element.93), channel_id=1, replica_groups=mesh['res_0'=4,'res_1'=4,'res_2'=2,'grp'=4] {'grp'}, use_global_device_ids=true, to_apply=%region_4.5 | all-reduce | flops 2 | bytes 16 | tf_op jit(solution)/shard_map/psum | solution.py:34
  156.2 10.9 %gather_fusion.1 = f32[2048,3]{1,0:T(8,128)} fusion(f32[3,16384]{0,1:T(8,128)} %bitcast.280, s32[2048]{0:T(1024)S(1)} %broadcast_clamp_fusion), kind=kCustom, calls=%fused_computation.1 | custom fusion | bytes 57344 | tf_op jit(solution)/shard_map/gather | solution.py:100
  190.4 17.3 %scatter_fusion.1 = f32[3,16384]{0,1:T(8,128)} fusion(f32[3,16384]{0,1:T(8,128)} %bitcast.269, s32[2048]{0:T(1024)S(1)} %bitcast.300, f32[2048,3]{1,0:T(8,128)} %bitcast.288), kind=kCustom, calls=%fused_computation.7 | custom fusion | flops 6144 | bytes 81920 | tf_op jit(solution)/shard_map/scatter-add | solution.py:105
  220.6 8.4 %all-reduce.28 = (f32[]{:T(128)}, f32[]{:T(128)}, f32[]{:T(128)}, f32[]{:T(128)}) all-reduce(f32[]{:T(128)} %get-tuple-element.43, f32[]{:T(128)} %get-tuple-element.42, f32[]{:T(128)} %multiply_reduce_fusion.2, f32[]{:T(128)} %get-tuple-element.41), channel_id=1, replica_groups=mesh['res_0'=4,'res_1'=4,'res_2'=2,'grp'=4] {'res_0'}, use_global_device_ids=true, to_apply=%region_41.42 | all-reduce | flops 4 | bytes 32 | tf_op jit(solution)/shard_map/psum | solution.py:34
  229.1 11.5 %all-reduce.24 = (f32[]{:T(128)}, f32[]{:T(128)}, f32[]{:T(128)}, f32[]{:T(128)}) all-reduce(f32[]{:T(128)} %get-tuple-element.76, f32[]{:T(128)} %get-tuple-element.77, f32[]{:T(128)} %get-tuple-element.78, f32[]{:T(128)} %get-tuple-element.79), channel_id=1, replica_groups=mesh['res_0'=4,'res_1'=4,'res_2'=2,'grp'=4] {'res_1'}, use_global_device_ids=true, to_apply=%region_42.43 | all-reduce | flops 4 | bytes 32 | tf_op jit(solution)/shard_map/psum | solution.py:34
  278.2 10.9 %gather_fusion.2 = f32[2048,3]{1,0:T(8,128)} fusion(f32[3,16384]{0,1:T(8,128)} %bitcast.281, s32[2048]{0:T(1024)S(1)} %broadcast_clamp_fusion), kind=kCustom, calls=%fused_computation.2 | custom fusion | bytes 57344 | tf_op jit(solution)/shard_map/gather | solution.py:100
  312.6 17.3 %scatter_fusion.2 = f32[3,16384]{0,1:T(8,128)} fusion(f32[3,16384]{0,1:T(8,128)} %bitcast.275, s32[2048]{0:T(1024)S(1)} %bitcast.301, f32[2048,3]{1,0:T(8,128)} %bitcast.289), kind=kCustom, calls=%fused_computation.8 | custom fusion | flops 6144 | bytes 81920 | tf_op jit(solution)/shard_map/scatter-add | solution.py:105
  337.4 8.9 %psum.416 = f32[]{:T(128)} all-reduce(f32[]{:T(128)} %multiply_reduce_fusion.14), channel_id=1, replica_groups=mesh['res_0'=4,'res_1'=4,'res_2'=2,'grp'=4] {'res_0'}, use_global_device_ids=true, to_apply=%region_60.61 | all-reduce | flops 1 | bytes 8 | tf_op jit(solution)/shard_map/psum | solution.py:34
  346.3 11.5 %psum.417 = f32[]{:T(128)} all-reduce(f32[]{:T(128)} %psum.416), channel_id=1, replica_groups=mesh['res_0'=4,'res_1'=4,'res_2'=2,'grp'=4] {'res_1'}, use_global_device_ids=true, to_apply=%region_61.62 | all-reduce | flops 1 | bytes 8 | tf_op jit(solution)/shard_map/psum | solution.py:34
  390.2 10.9 %gather_fusion.3 = f32[2048,3]{1,0:T(8,128)} fusion(f32[3,16384]{0,1:T(8,128)} %bitcast.282, s32[2048]{0:T(1024)S(1)} %broadcast_clamp_fusion), kind=kCustom, calls=%fused_computation.3 | custom fusion | bytes 57344 | tf_op jit(solution)/shard_map/gather | solution.py:100
  424.4 17.3 %scatter_fusion.3 = f32[3,16384]{0,1:T(8,128)} fusion(f32[3,16384]{0,1:T(8,128)} %bitcast.271, s32[2048]{0:T(1024)S(1)} %bitcast.302, f32[2048,3]{1,0:T(8,128)} %bitcast.290), kind=kCustom, calls=%fused_computation.9 | custom fusion | flops 6144 | bytes 81920 | tf_op jit(solution)/shard_map/scatter-add | solution.py:105
  454.7 8.4 %all-reduce.27 = (f32[]{:T(128)}, f32[]{:T(128)}, f32[]{:T(128)}, f32[]{:T(128)}) all-reduce(f32[]{:T(128)} %get-tuple-element.40, f32[]{:T(128)} %get-tuple-element.39, f32[]{:T(128)} %multiply_reduce_fusion.1, f32[]{:T(128)} %get-tuple-element.38), channel_id=1, replica_groups=mesh['res_0'=4,'res_1'=4,'res_2'=2,'grp'=4] {'res_0'}, use_global_device_ids=true, to_apply=%region_84.85 | all-reduce | flops 4 | bytes 32 | tf_op jit(solution)/shard_map/psum | solution.py:34
  463.1 11.2 %all-reduce.23 = (f32[]{:T(128)}, f32[]{:T(128)}, f32[]{:T(128)}, f32[]{:T(128)}) all-reduce(f32[]{:T(128)} %get-tuple-element.72, f32[]{:T(128)} %get-tuple-element.73, f32[]{:T(128)} %get-tuple-element.74, f32[]{:T(128)} %get-tuple-element.75), channel_id=1, replica_groups=mesh['res_0'=4,'res_1'=4,'res_2'=2,'grp'=4] {'res_1'}, use_global_device_ids=true, to_apply=%region_85.86 | all-reduce | flops 4 | bytes 32 | tf_op jit(solution)/shard_map/psum | solution.py:34
  510.9 10.9 %gather_fusion.4 = f32[2048,3]{1,0:T(8,128)} fusion(f32[3,16384]{0,1:T(8,128)} %bitcast.283, s32[2048]{0:T(1024)S(1)} %broadcast_clamp_fusion), kind=kCustom, calls=%fused_computation.4 | custom fusion | bytes 57344 | tf_op jit(solution)/shard_map/gather | solution.py:100
  545.1 17.3 %scatter_fusion.4 = f32[3,16384]{0,1:T(8,128)} fusion(f32[3,16384]{0,1:T(8,128)} %bitcast.277, s32[2048]{0:T(1024)S(1)} %bitcast.303, f32[2048,3]{1,0:T(8,128)} %bitcast.286), kind=kCustom, calls=%fused_computation.10 | custom fusion | flops 6144 | bytes 81920 | tf_op jit(solution)/shard_map/scatter-add | solution.py:105
  578.4 11.9 %psum.437 = f32[]{:T(128)} all-reduce(f32[]{:T(128)} %psum.436), channel_id=1, replica_groups=mesh['res_0'=4,'res_1'=4,'res_2'=2,'grp'=4] {'res_1'}, use_global_device_ids=true, to_apply=%region_104.105 | all-reduce | flops 1 | bytes 8 | tf_op jit(solution)/shard_map/psum | solution.py:34
  622.3 10.9 %gather_fusion.5 = f32[2048,3]{1,0:T(8,128)} fusion(f32[3,16384]{0,1:T(8,128)} %bitcast.279, s32[2048]{0:T(1024)S(1)} %broadcast_clamp_fusion), kind=kCustom, calls=%fused_computation.5 | custom fusion | bytes 57344 | tf_op jit(solution)/shard_map/gather | solution.py:100
  654.9 17.3 %scatter_fusion.5 = f32[3,16384]{0,1:T(8,128)} fusion(f32[3,16384]{0,1:T(8,128)} %bitcast.267, s32[2048]{0:T(1024)S(1)} %bitcast.304, f32[2048,3]{1,0:T(8,128)} %bitcast.287), kind=kCustom, calls=%fused_computation.11 | custom fusion | flops 6144 | bytes 81920 | tf_op jit(solution)/shard_map/scatter-add | solution.py:105
  691.7 11.0 %all-reduce.22 = (f32[]{:T(128)}, f32[]{:T(128)}) all-reduce(f32[]{:T(128)} %get-tuple-element.70, f32[]{:T(128)} %get-tuple-element.71), channel_id=1, replica_groups=mesh['res_0'=4,'res_1'=4,'res_2'=2,'grp'=4] {'res_1'}, use_global_device_ids=true, to_apply=%region_118.119 | all-reduce | flops 2 | bytes 16 | tf_op jit(solution)/shard_map/psum | solution.py:34
  705.7 11.0 %all-reduce.18 = (f32[]{:T(128)}, f32[]{:T(128)}) all-reduce(f32[]{:T(128)} %get-tuple-element.82, f32[]{:T(128)} %get-tuple-element.83), channel_id=1, replica_groups=mesh['res_0'=4,'res_1'=4,'res_2'=2,'grp'=4] {'grp'}, use_global_device_ids=true, to_apply=%region_120.121 | all-reduce | flops 2 | bytes 16 | tf_op jit(solution)/shard_map/psum | solution.py:34
  (218 shorter events, 408.0 us)
Async XLA Ops:
  0.7 60.2 %all-to-all-start = ((f32[4,4,256,256]{3,2,1,0:T(8,128)}), f32[4,4,256,256]{3,2,1,0:T(8,128)}, u32[]{:S(2)}, u32[]{:S(2)}) async-start(f32[4,4,256,256]{3,2,1,0:T(8,128)} %bitcast.285), calls=%async_computation | async-start | bytes 8388608 | tf_op jit(solution)/shard_map/all_to_all | solution.py:89
  7.8 45.1 %collective-permute-start.3 = (f32[3,2,1,512]{3,2,1,0:T(1,128)}, f32[3,2,1,512]{3,2,1,0:T(1,128)}, u32[]{:S(2)}, u32[]{:S(2)}) collective-permute-start(f32[3,2,1,512]{3,2,1,0:T(1,128)} %get-tuple-element.171), channel_id=1, source_target_pairs={{0,1},{1,2},{2,3},{4,5},{5,6},{6,7},{8,9},{9,10},{10,11},{12,13},{... | collective-permute-start | bytes 36872 | tf_op jit(solution)/shard_map/ppermute | solution.py:20
  11.2 41.8 %collective-permute-start.2 = (f32[3,2,1,512]{3,2,1,0:T(1,128)}, f32[3,2,1,512]{3,2,1,0:T(1,128)}, u32[]{:S(2)}, u32[]{:S(2)}) collective-permute-start(f32[3,2,1,512]{3,2,1,0:T(1,128)} %get-tuple-element.172), channel_id=1, source_target_pairs={{1,0},{2,1},{3,2},{5,4},{6,5},{7,6},{9,8},{10,9},{11,10},{13,12},{... | collective-permute-start | bytes 36872 | tf_op jit(solution)/shard_map/ppermute | solution.py:21
  15.9 33.6 %collective-permute-start.1 = (f32[3,1,16,512]{3,2,1,0:T(8,128)}, f32[3,1,16,512]{3,2,1,0:T(8,128)}, u32[]{:S(2)}, u32[]{:S(2)}) collective-permute-start(f32[3,1,16,512]{3,2,1,0:T(8,128)} %get-tuple-element.173), channel_id=1, source_target_pairs={{0,4},{4,8},{8,12},{12,16},{16,20},{20,24},{24,28},{28,32},{32,36}... | collective-permute-start | bytes 294920 | tf_op jit(solution)/shard_map/ppermute | solution.py:20
  17.8 32.6 %collective-permute-start = (f32[3,1,16,512]{3,2,1,0:T(8,128)}, f32[3,1,16,512]{3,2,1,0:T(8,128)}, u32[]{:S(2)}, u32[]{:S(2)}) collective-permute-start(f32[3,1,16,512]{3,2,1,0:T(8,128)} %get-tuple-element.174), channel_id=1, source_target_pairs={{4,0},{8,4},{12,8},{16,12},{20,16},{24,20},{28,24},{32,28},{36,32}... | collective-permute-start | bytes 294920 | tf_op jit(solution)/shard_map/ppermute | solution.py:21
  143.9 36.9 %collective-permute-start.7 = (f32[3,2,1,512]{3,2,1,0:T(1,128)}, f32[3,2,1,512]{3,2,1,0:T(1,128)}, u32[]{:S(2)}, u32[]{:S(2)}) collective-permute-start(f32[3,2,1,512]{3,2,1,0:T(1,128)} %get-tuple-element.162), channel_id=1, source_target_pairs={{0,1},{1,2},{2,3},{4,5},{5,6},{6,7},{8,9},{9,10},{10,11},{12,13},{... | collective-permute-start | bytes 36872 | tf_op jit(solution)/shard_map/ppermute | solution.py:20
  147.5 33.2 %collective-permute-start.6 = (f32[3,2,1,512]{3,2,1,0:T(1,128)}, f32[3,2,1,512]{3,2,1,0:T(1,128)}, u32[]{:S(2)}, u32[]{:S(2)}) collective-permute-start(f32[3,2,1,512]{3,2,1,0:T(1,128)} %get-tuple-element.163), channel_id=1, source_target_pairs={{1,0},{2,1},{3,2},{5,4},{6,5},{7,6},{9,8},{10,9},{11,10},{13,12},{... | collective-permute-start | bytes 36872 | tf_op jit(solution)/shard_map/ppermute | solution.py:21
  150.6 30.1 %collective-permute-start.5 = (f32[3,1,16,512]{3,2,1,0:T(8,128)}, f32[3,1,16,512]{3,2,1,0:T(8,128)}, u32[]{:S(2)}, u32[]{:S(2)}) collective-permute-start(f32[3,1,16,512]{3,2,1,0:T(8,128)} %get-tuple-element.164), channel_id=1, source_target_pairs={{0,4},{4,8},{8,12},{12,16},{16,20},{20,24},{24,28},{28,32},{32,36}... | collective-permute-start | bytes 294920 | tf_op jit(solution)/shard_map/ppermute | solution.py:20
  265.9 36.8 %collective-permute-start.11 = (f32[3,2,1,512]{3,2,1,0:T(1,128)}, f32[3,2,1,512]{3,2,1,0:T(1,128)}, u32[]{:S(2)}, u32[]{:S(2)}) collective-permute-start(f32[3,2,1,512]{3,2,1,0:T(1,128)} %get-tuple-element.152), channel_id=1, source_target_pairs={{0,1},{1,2},{2,3},{4,5},{5,6},{6,7},{8,9},{9,10},{10,11},{12,13},{... | collective-permute-start | bytes 36872 | tf_op jit(solution)/shard_map/ppermute | solution.py:20
  269.0 33.7 %collective-permute-start.10 = (f32[3,2,1,512]{3,2,1,0:T(1,128)}, f32[3,2,1,512]{3,2,1,0:T(1,128)}, u32[]{:S(2)}, u32[]{:S(2)}) collective-permute-start(f32[3,2,1,512]{3,2,1,0:T(1,128)} %get-tuple-element.153), channel_id=1, source_target_pairs={{1,0},{2,1},{3,2},{5,4},{6,5},{7,6},{9,8},{10,9},{11,10},{13,12},{... | collective-permute-start | bytes 36872 | tf_op jit(solution)/shard_map/ppermute | solution.py:21
  272.4 30.4 %collective-permute-start.9 = (f32[3,1,16,512]{3,2,1,0:T(8,128)}, f32[3,1,16,512]{3,2,1,0:T(8,128)}, u32[]{:S(2)}, u32[]{:S(2)}) collective-permute-start(f32[3,1,16,512]{3,2,1,0:T(8,128)} %get-tuple-element.154), channel_id=1, source_target_pairs={{0,4},{4,8},{8,12},{12,16},{16,20},{20,24},{24,28},{28,32},{32,36}... | collective-permute-start | bytes 294920 | tf_op jit(solution)/shard_map/ppermute | solution.py:20
  274.3 28.4 %collective-permute-start.8 = (f32[3,1,16,512]{3,2,1,0:T(8,128)}, f32[3,1,16,512]{3,2,1,0:T(8,128)}, u32[]{:S(2)}, u32[]{:S(2)}) collective-permute-start(f32[3,1,16,512]{3,2,1,0:T(8,128)} %get-tuple-element.155), channel_id=1, source_target_pairs={{4,0},{8,4},{12,8},{16,12},{20,16},{24,20},{28,24},{32,28},{36,32}... | collective-permute-start | bytes 294920 | tf_op jit(solution)/shard_map/ppermute | solution.py:21
  377.9 36.8 %collective-permute-start.15 = (f32[3,2,1,512]{3,2,1,0:T(1,128)}, f32[3,2,1,512]{3,2,1,0:T(1,128)}, u32[]{:S(2)}, u32[]{:S(2)}) collective-permute-start(f32[3,2,1,512]{3,2,1,0:T(1,128)} %get-tuple-element.142), channel_id=1, source_target_pairs={{0,1},{1,2},{2,3},{4,5},{5,6},{6,7},{8,9},{9,10},{10,11},{12,13},{... | collective-permute-start | bytes 36872 | tf_op jit(solution)/shard_map/ppermute | solution.py:20
  380.9 33.8 %collective-permute-start.14 = (f32[3,2,1,512]{3,2,1,0:T(1,128)}, f32[3,2,1,512]{3,2,1,0:T(1,128)}, u32[]{:S(2)}, u32[]{:S(2)}) collective-permute-start(f32[3,2,1,512]{3,2,1,0:T(1,128)} %get-tuple-element.143), channel_id=1, source_target_pairs={{1,0},{2,1},{3,2},{5,4},{6,5},{7,6},{9,8},{10,9},{11,10},{13,12},{... | collective-permute-start | bytes 36872 | tf_op jit(solution)/shard_map/ppermute | solution.py:21
  384.4 30.4 %collective-permute-start.13 = (f32[3,1,16,512]{3,2,1,0:T(8,128)}, f32[3,1,16,512]{3,2,1,0:T(8,128)}, u32[]{:S(2)}, u32[]{:S(2)}) collective-permute-start(f32[3,1,16,512]{3,2,1,0:T(8,128)} %get-tuple-element.144), channel_id=1, source_target_pairs={{0,4},{4,8},{8,12},{12,16},{16,20},{20,24},{24,28},{28,32},{32,36}... | collective-permute-start | bytes 294920 | tf_op jit(solution)/shard_map/ppermute | solution.py:20
  386.3 28.5 %collective-permute-start.12 = (f32[3,1,16,512]{3,2,1,0:T(8,128)}, f32[3,1,16,512]{3,2,1,0:T(8,128)}, u32[]{:S(2)}, u32[]{:S(2)}) collective-permute-start(f32[3,1,16,512]{3,2,1,0:T(8,128)} %get-tuple-element.145), channel_id=1, source_target_pairs={{4,0},{8,4},{12,8},{16,12},{20,16},{24,20},{28,24},{32,28},{36,32}... | collective-permute-start | bytes 294920 | tf_op jit(solution)/shard_map/ppermute | solution.py:21
  498.5 37.0 %collective-permute-start.19 = (f32[3,2,1,512]{3,2,1,0:T(1,128)}, f32[3,2,1,512]{3,2,1,0:T(1,128)}, u32[]{:S(2)}, u32[]{:S(2)}) collective-permute-start(f32[3,2,1,512]{3,2,1,0:T(1,128)} %get-tuple-element.132), channel_id=1, source_target_pairs={{0,1},{1,2},{2,3},{4,5},{5,6},{6,7},{8,9},{9,10},{10,11},{12,13},{... | collective-permute-start | bytes 36872 | tf_op jit(solution)/shard_map/ppermute | solution.py:20
  501.4 34.0 %collective-permute-start.18 = (f32[3,2,1,512]{3,2,1,0:T(1,128)}, f32[3,2,1,512]{3,2,1,0:T(1,128)}, u32[]{:S(2)}, u32[]{:S(2)}) collective-permute-start(f32[3,2,1,512]{3,2,1,0:T(1,128)} %get-tuple-element.133), channel_id=1, source_target_pairs={{1,0},{2,1},{3,2},{5,4},{6,5},{7,6},{9,8},{10,9},{11,10},{13,12},{... | collective-permute-start | bytes 36872 | tf_op jit(solution)/shard_map/ppermute | solution.py:21
  504.9 30.6 %collective-permute-start.17 = (f32[3,1,16,512]{3,2,1,0:T(8,128)}, f32[3,1,16,512]{3,2,1,0:T(8,128)}, u32[]{:S(2)}, u32[]{:S(2)}) collective-permute-start(f32[3,1,16,512]{3,2,1,0:T(8,128)} %get-tuple-element.134), channel_id=1, source_target_pairs={{0,4},{4,8},{8,12},{12,16},{16,20},{20,24},{24,28},{28,32},{32,36}... | collective-permute-start | bytes 294920 | tf_op jit(solution)/shard_map/ppermute | solution.py:20
  506.8 28.7 %collective-permute-start.16 = (f32[3,1,16,512]{3,2,1,0:T(8,128)}, f32[3,1,16,512]{3,2,1,0:T(8,128)}, u32[]{:S(2)}, u32[]{:S(2)}) collective-permute-start(f32[3,1,16,512]{3,2,1,0:T(8,128)} %get-tuple-element.135), channel_id=1, source_target_pairs={{4,0},{8,4},{12,8},{16,12},{20,16},{24,20},{28,24},{32,28},{36,32}... | collective-permute-start | bytes 294920 | tf_op jit(solution)/shard_map/ppermute | solution.py:21
  610.4 36.5 %collective-permute-start.22 = (f32[3,2,1,512]{3,2,1,0:T(1,128)}, f32[3,2,1,512]{3,2,1,0:T(1,128)}, u32[]{:S(2)}, u32[]{:S(2)}) collective-permute-start(f32[3,2,1,512]{3,2,1,0:T(1,128)} %get-tuple-element.122), channel_id=1, source_target_pairs={{1,0},{2,1},{3,2},{5,4},{6,5},{7,6},{9,8},{10,9},{11,10},{13,12},{... | collective-permute-start | bytes 36872 | tf_op jit(solution)/shard_map/ppermute | solution.py:21
  614.6 32.3 %collective-permute-start.23 = (f32[3,2,1,512]{3,2,1,0:T(1,128)}, f32[3,2,1,512]{3,2,1,0:T(1,128)}, u32[]{:S(2)}, u32[]{:S(2)}) collective-permute-start(f32[3,2,1,512]{3,2,1,0:T(1,128)} %get-tuple-element.123), channel_id=1, source_target_pairs={{0,1},{1,2},{2,3},{4,5},{5,6},{6,7},{8,9},{9,10},{10,11},{12,13},{... | collective-permute-start | bytes 36872 | tf_op jit(solution)/shard_map/ppermute | solution.py:20
  616.5 30.4 %collective-permute-start.21 = (f32[3,1,16,512]{3,2,1,0:T(8,128)}, f32[3,1,16,512]{3,2,1,0:T(8,128)}, u32[]{:S(2)}, u32[]{:S(2)}) collective-permute-start(f32[3,1,16,512]{3,2,1,0:T(8,128)} %get-tuple-element.124), channel_id=1, source_target_pairs={{0,4},{4,8},{8,12},{12,16},{16,20},{20,24},{24,28},{28,32},{32,36}... | collective-permute-start | bytes 294920 | tf_op jit(solution)/shard_map/ppermute | solution.py:20
  618.5 28.5 %collective-permute-start.20 = (f32[3,1,16,512]{3,2,1,0:T(8,128)}, f32[3,1,16,512]{3,2,1,0:T(8,128)}, u32[]{:S(2)}, u32[]{:S(2)}) collective-permute-start(f32[3,1,16,512]{3,2,1,0:T(8,128)} %get-tuple-element.125), channel_id=1, source_target_pairs={{4,0},{8,4},{12,8},{16,12},{20,16},{24,20},{28,24},{32,28},{36,32}... | collective-permute-start | bytes 294920 | tf_op jit(solution)/shard_map/ppermute | solution.py:21
  (18 other events, 411.7 us)
where the time goes:
time: 734 us; the launch traced here: 719 us
  local copies, waits for them, and re-layouts  205 us (28%)
  other arithmetic  196 us (27%)
  blocking collectives  194 us (26%)
  starting transfers between devices  78.5 us (11%)
  matrix products  28.8 us (4%)
  between operations  15.8 us (2%)
    psum x24, blocking collectives, over_axes(): shard = lax.psum(shard, axis)  194 us
    scatter-add x6, other arithmetic, operator(): out_flat = result.reshape(components, -1).at[:, flat_index].add(-correction)  104 us
    gather x6, local copies, waits for them, and re-layouts, operator(): flat[:, flat_index].reshape(components, blocks, segb)  65.7 us
    ppermute x12, starting transfers between devices, extended(): lax.ppermute(leading, axis, [(b, a) for a, b in up])  43.5 us
    reshape x6, local copies, waits for them, and re-layouts, operator(): return out_flat.reshape(vector.shape)  34.5 us
    sub x6, local copies, waits for them, and re-layouts, stencil(): result - jnp.sum(transmissibility[face] * beside_list[face][None], axis=1)  32.8 us
    ppermute x12, starting transfers between devices, extended(): lax.ppermute(last, axis, up)  29.4 us
    dot_general x6, matrix products, solve_wells(): return jnp.einsum('bst,bt->bs', block_inverse, coupled, precision=highest)  22.8 us
  transfers between devices with their start and end apart: 25, of which 0 were waited for; matrix products, arithmetic and copies ran while one was open for 23% of the time, Pallas kernels for 0%

commit v1 on v0

--- a/solution.py
+++ b/solution.py
@@ -31,7 +31,8 @@
 
 def over_axes(shard, axes):
     for axis in axes:
-        shard = lax.psum(shard, axis)
+        pieces = lax.all_gather(shard, axis)
+        shard = jnp.sum(pieces, axis=0)
     return shard
 
 

time: 734 us -> 971 us (1.32)
  local copies, waits for them, and re-layouts: 205 us -> 377 us
  other arithmetic: 196 us -> 268 us
  starting transfers between devices: 78.5 us -> 68.2 us
    psum x24 -> x0, blocking collectives: 194 us -> none  [over_axes(): shard = lax.psum(shard, axis)]
    unnamed x0 -> x24, blocking collectives: none -> 194 us
    unnamed x37 -> x145, local copies, waits for them, and re-layouts: 8 us -> 170 us
    reduce_sum x0 -> x56, other arithmetic: none -> 67.5 us  [over_axes(): shard = jnp.sum(pieces, axis=0)]
    ppermute x12, starting transfers between devices: 43.5 us -> 28.6 us  [extended(): lax.ppermute(leading, axis, [(b, a) for a, b in up])]
  transfers between devices with their start and end apart: 25 -> 25, of which waited for: 0 -> 0; matrix products, arithmetic and copies ran while one was open for 23% -> 7% of each run, Pallas kernels for 0% -> 0%
where the time goes in v1:
time: 971 us; the launch traced here: 953 us
  local copies, waits for them, and re-layouts  377 us (39%)
  other arithmetic  268 us (28%)
  blocking collectives  194 us (20%)
  starting transfers between devices  68.2 us (7%)
  matrix products  28.8 us (3%)
  between operations  16.6 us (2%)
    unnamed x24, blocking collectives  194 us
    unnamed x145, local copies, waits for them, and re-layouts  170 us
    scatter-add x6, other arithmetic, operator(): out_flat = result.reshape(components, -1).at[:, flat_index].add(-correction)  104 us
    reduce_sum x56, other arithmetic, over_axes(): shard = jnp.sum(pieces, axis=0)  67.5 us
    gather x6, local copies, waits for them, and re-layouts, operator(): flat[:, flat_index].reshape(components, blocks, segb)  65.6 us
    reshape x6, local copies, waits for them, and re-layouts, operator(): return out_flat.reshape(vector.shape)  34.5 us
    ppermute x12, starting transfers between devices, extended(): lax.ppermute(last, axis, up)  34 us
    sub x6, local copies, waits for them, and re-layouts, stencil(): result - jnp.sum(transmissibility[face] * beside_list[face][None], axis=1)  32.8 us
  transfers between devices with their start and end apart: 25, of which 0 were waited for; matrix products, arithmetic and copies ran while one was open for 7% of the time, Pallas kernels for 0%

profile of v1, /device:TPU:10, one launch (start us, length us, event | category | flops | bytes accessed | tf_op | source)
XLA Modules:
  0.0 952.8 jit_solution(675561980886700099)
XLA Ops:
  26.6 11.0 %gather_fusion = f32[2048,3]{1,0:T(8,128)} fusion(f32[3,16384]{0,1:T(8,128)} %bitcast.344, s32[2048]{0:T(1024)S(1)} %broadcast_clamp_fusion), kind=kCustom, calls=%fused_computation | custom fusion | bytes 57344 | tf_op jit(solution)/shard_map/gather | solution.py:101
  75.7 17.5 %scatter_fusion = f32[3,16384]{0,1:T(8,128)} fusion(f32[3,16384]{0,1:T(8,128)} %bitcast.333, s32[2048]{0:T(1024)S(1)} %bitcast.359, f32[2048,3]{1,0:T(8,128)} %bitcast.351), kind=kCustom, calls=%fused_computation.6 | custom fusion | flops 6144 | bytes 81920 | tf_op jit(solution)/shard_map/scatter-add | solution.py:106
  108.3 12.5 %all-reduce.85 = (f32[4]{0:T(128)}, f32[4]{0:T(128)}) all-reduce(f32[4]{0:T(128)} %dynamic-update-slice, f32[4]{0:T(128)} %dynamic-update-slice.4), channel_id=1, replica_groups=mesh['res_0'=4,'res_1'=4,'res_2'=2,'grp'=4] {'res_0'}, use_global_device_ids=true, to_apply=%add.18 | all-reduce | flops 8 | bytes 64
  130.8 11.1 %all-reduce.81 = (f32[4]{0:T(128)}, f32[4]{0:T(128)}) all-reduce(f32[4]{0:T(128)} %dynamic-update-slice.1, f32[4]{0:T(128)} %dynamic-update-slice.5), channel_id=1, replica_groups=mesh['res_0'=4,'res_1'=4,'res_2'=2,'grp'=4] {'res_1'}, use_global_device_ids=true, to_apply=%add.19 | all-reduce | flops 8 | bytes 64
  164.1 9.8 %all-reduce.77 = (f32[4]{0:T(128)}, f32[4]{0:T(128)}) all-reduce(f32[4]{0:T(128)} %dynamic-update-slice.3, f32[4]{0:T(128)} %dynamic-update-slice.7), channel_id=1, replica_groups=mesh['res_0'=4,'res_1'=4,'res_2'=2,'grp'=4] {'grp'}, use_global_device_ids=true, to_apply=%add.21 | all-reduce | flops 8 | bytes 64
  188.5 10.9 %gather_fusion.1 = f32[2048,3]{1,0:T(8,128)} fusion(f32[3,16384]{0,1:T(8,128)} %bitcast.340, s32[2048]{0:T(1024)S(1)} %broadcast_clamp_fusion), kind=kCustom, calls=%fused_computation.1 | custom fusion | bytes 57344 | tf_op jit(solution)/shard_map/gather | solution.py:101
  232.9 17.3 %scatter_fusion.1 = f32[3,16384]{0,1:T(8,128)} fusion(f32[3,16384]{0,1:T(8,128)} %bitcast.329, s32[2048]{0:T(1024)S(1)} %bitcast.360, f32[2048,3]{1,0:T(8,128)} %bitcast.348), kind=kCustom, calls=%fused_computation.7 | custom fusion | flops 6144 | bytes 81920 | tf_op jit(solution)/shard_map/scatter-add | solution.py:106
  300.6 9.7 %all-reduce.80 = (f32[4]{0:T(128)}, f32[4]{0:T(128)}, f32[4]{0:T(128)}, f32[4]{0:T(128)}) all-reduce(f32[4]{0:T(128)} %dynamic-update-slice.17, f32[4]{0:T(128)} %dynamic-update-slice.9, f32[4]{0:T(128)} %dynamic-update-slice.13, f32[4]{0:T(128)} %dynamic-update-slice.21), channel_id=1, replica_groups=mesh['res_0'=4,'res_1'=4,'res_2'=2,'grp'=4] {'res_1'}, use_global_device_ids=true, to_apply=%add.35 | all-reduce | flops 16 | bytes 128
  347.7 10.0 %all-reduce.76 = (f32[4]{0:T(128)}, f32[4]{0:T(128)}, f32[4]{0:T(128)}, f32[4]{0:T(128)}) all-reduce(f32[4]{0:T(128)} %dynamic-update-slice.19, f32[4]{0:T(128)} %dynamic-update-slice.11, f32[4]{0:T(128)} %dynamic-update-slice.15, f32[4]{0:T(128)} %dynamic-update-slice.23), channel_id=1, replica_groups=mesh['res_0'=4,'res_1'=4,'res_2'=2,'grp'=4] {'grp'}, use_global_device_ids=true, to_apply=%add.37 | all-reduce | flops 16 | bytes 128
  379.5 10.9 %gather_fusion.2 = f32[2048,3]{1,0:T(8,128)} fusion(f32[3,16384]{0,1:T(8,128)} %bitcast.341, s32[2048]{0:T(1024)S(1)} %broadcast_clamp_fusion), kind=kCustom, calls=%fused_computation.2 | custom fusion | bytes 57344 | tf_op jit(solution)/shard_map/gather | solution.py:101
  424.1 17.3 %scatter_fusion.2 = f32[3,16384]{0,1:T(8,128)} fusion(f32[3,16384]{0,1:T(8,128)} %bitcast.335, s32[2048]{0:T(1024)S(1)} %bitcast.361, f32[2048,3]{1,0:T(8,128)} %bitcast.349), kind=kCustom, calls=%fused_computation.8 | custom fusion | flops 6144 | bytes 81920 | tf_op jit(solution)/shard_map/scatter-add | solution.py:106
  452.2 10.4 %all-reduce.42 = f32[4]{0:T(128)} all-reduce(f32[4]{0:T(128)} %dynamic-update-slice.24), channel_id=1, replica_groups=mesh['res_0'=4,'res_1'=4,'res_2'=2,'grp'=4] {'res_0'}, use_global_device_ids=true, to_apply=%add.42 | all-reduce | flops 4 | bytes 32
  488.5 9.8 %all-reduce.45 = f32[4]{0:T(128)} all-reduce(f32[4]{0:T(128)} %dynamic-update-slice.27), channel_id=1, replica_groups=mesh['res_0'=4,'res_1'=4,'res_2'=2,'grp'=4] {'grp'}, use_global_device_ids=true, to_apply=%add.45 | all-reduce | flops 4 | bytes 32
  511.1 10.9 %gather_fusion.3 = f32[2048,3]{1,0:T(8,128)} fusion(f32[3,16384]{0,1:T(8,128)} %bitcast.342, s32[2048]{0:T(1024)S(1)} %broadcast_clamp_fusion), kind=kCustom, calls=%fused_computation.3 | custom fusion | bytes 57344 | tf_op jit(solution)/shard_map/gather | solution.py:101
  555.7 17.3 %scatter_fusion.3 = f32[3,16384]{0,1:T(8,128)} fusion(f32[3,16384]{0,1:T(8,128)} %bitcast.331, s32[2048]{0:T(1024)S(1)} %bitcast.362, f32[2048,3]{1,0:T(8,128)} %bitcast.350), kind=kCustom, calls=%fused_computation.9 | custom fusion | flops 6144 | bytes 81920 | tf_op jit(solution)/shard_map/scatter-add | solution.py:106
  624.5 10.0 %all-reduce.79 = (f32[4]{0:T(128)}, f32[4]{0:T(128)}, f32[4]{0:T(128)}, f32[4]{0:T(128)}) all-reduce(f32[4]{0:T(128)} %dynamic-update-slice.37, f32[4]{0:T(128)} %dynamic-update-slice.29, f32[4]{0:T(128)} %dynamic-update-slice.33, f32[4]{0:T(128)} %dynamic-update-slice.41), channel_id=1, replica_groups=mesh['res_0'=4,'res_1'=4,'res_2'=2,'grp'=4] {'res_1'}, use_global_device_ids=true, to_apply=%add.55 | all-reduce | flops 16 | bytes 128
  672.1 9.6 %all-reduce.75 = (f32[4]{0:T(128)}, f32[4]{0:T(128)}, f32[4]{0:T(128)}, f32[4]{0:T(128)}) all-reduce(f32[4]{0:T(128)} %dynamic-update-slice.39, f32[4]{0:T(128)} %dynamic-update-slice.31, f32[4]{0:T(128)} %dynamic-update-slice.35, f32[4]{0:T(128)} %dynamic-update-slice.43), channel_id=1, replica_groups=mesh['res_0'=4,'res_1'=4,'res_2'=2,'grp'=4] {'grp'}, use_global_device_ids=true, to_apply=%add.57 | all-reduce | flops 16 | bytes 128
  702.6 10.9 %gather_fusion.4 = f32[2048,3]{1,0:T(8,128)} fusion(f32[3,16384]{0,1:T(8,128)} %bitcast.343, s32[2048]{0:T(1024)S(1)} %broadcast_clamp_fusion), kind=kCustom, calls=%fused_computation.4 | custom fusion | bytes 57344 | tf_op jit(solution)/shard_map/gather | solution.py:101
  747.2 17.3 %scatter_fusion.4 = f32[3,16384]{0,1:T(8,128)} fusion(f32[3,16384]{0,1:T(8,128)} %bitcast.337, s32[2048]{0:T(1024)S(1)} %bitcast.363, f32[2048,3]{1,0:T(8,128)} %bitcast.346), kind=kCustom, calls=%fused_computation.10 | custom fusion | flops 6144 | bytes 81920 | tf_op jit(solution)/shard_map/scatter-add | solution.py:106
  775.3 10.4 %all-reduce.62 = f32[4]{0:T(128)} all-reduce(f32[4]{0:T(128)} %dynamic-update-slice.44), channel_id=1, replica_groups=mesh['res_0'=4,'res_1'=4,'res_2'=2,'grp'=4] {'res_0'}, use_global_device_ids=true, to_apply=%add.62 | all-reduce | flops 4 | bytes 32
  810.8 9.8 %all-reduce.65 = f32[4]{0:T(128)} all-reduce(f32[4]{0:T(128)} %dynamic-update-slice.47), channel_id=1, replica_groups=mesh['res_0'=4,'res_1'=4,'res_2'=2,'grp'=4] {'grp'}, use_global_device_ids=true, to_apply=%add.65 | all-reduce | flops 4 | bytes 32
  833.3 10.9 %gather_fusion.5 = f32[2048,3]{1,0:T(8,128)} fusion(f32[3,16384]{0,1:T(8,128)} %bitcast.339, s32[2048]{0:T(1024)S(1)} %broadcast_clamp_fusion), kind=kCustom, calls=%fused_computation.5 | custom fusion | bytes 57344 | tf_op jit(solution)/shard_map/gather | solution.py:101
  876.1 17.5 %scatter_fusion.5 = f32[3,16384]{0,1:T(8,128)} fusion(f32[3,16384]{0,1:T(8,128)} %bitcast.327, s32[2048]{0:T(1024)S(1)} %bitcast.364, f32[2048,3]{1,0:T(8,128)} %bitcast.347), kind=kCustom, calls=%fused_computation.11 | custom fusion | flops 6144 | bytes 81920 | tf_op jit(solution)/shard_map/scatter-add | solution.py:106
  907.6 9.4 all-reduce.82
  (382 shorter events, 644.1 us)
Async XLA Ops:
  0.7 61.7 %all-to-all-start = ((f32[4,4,256,256]{3,2,1,0:T(8,128)}), f32[4,4,256,256]{3,2,1,0:T(8,128)}, u32[]{:S(2)}, u32[]{:S(2)}) async-start(f32[4,4,256,256]{3,2,1,0:T(8,128)} %bitcast.345), calls=%async_computation | async-start | bytes 8388608 | tf_op jit(solution)/shard_map/all_to_all | solution.py:90
  7.9 43.1 %collective-permute-start.1 = (f32[3,1,16,512]{3,2,1,0:T(8,128)}, f32[3,1,16,512]{3,2,1,0:T(8,128)}, u32[]{:S(2)}, u32[]{:S(2)}) collective-permute-start(f32[3,1,16,512]{3,2,1,0:T(8,128)} %get-tuple-element.173), channel_id=1, source_target_pairs={{0,4},{4,8},{8,12},{12,16},{16,20},{20,24},{24,28},{28,32},{32,36}... | collective-permute-start | bytes 294920 | tf_op jit(solution)/shard_map/ppermute | solution.py:20
  9.8 42.0 %collective-permute-start = (f32[3,1,16,512]{3,2,1,0:T(8,128)}, f32[3,1,16,512]{3,2,1,0:T(8,128)}, u32[]{:S(2)}, u32[]{:S(2)}) collective-permute-start(f32[3,1,16,512]{3,2,1,0:T(8,128)} %get-tuple-element.174), channel_id=1, source_target_pairs={{4,0},{8,4},{12,8},{16,12},{20,16},{24,20},{28,24},{32,28},{36,32}... | collective-permute-start | bytes 294920 | tf_op jit(solution)/shard_map/ppermute | solution.py:21
  15.0 39.4 %collective-permute-start.2 = (f32[3,2,1,512]{3,2,1,0:T(1,128)}, f32[3,2,1,512]{3,2,1,0:T(1,128)}, u32[]{:S(2)}, u32[]{:S(2)}) collective-permute-start(f32[3,2,1,512]{3,2,1,0:T(1,128)} %get-tuple-element.172), channel_id=1, source_target_pairs={{1,0},{2,1},{3,2},{5,4},{6,5},{7,6},{9,8},{10,9},{11,10},{13,12},{... | collective-permute-start | bytes 36872 | tf_op jit(solution)/shard_map/ppermute | solution.py:21
  17.0 37.5 %collective-permute-start.3 = (f32[3,2,1,512]{3,2,1,0:T(1,128)}, f32[3,2,1,512]{3,2,1,0:T(1,128)}, u32[]{:S(2)}, u32[]{:S(2)}) collective-permute-start(f32[3,2,1,512]{3,2,1,0:T(1,128)} %get-tuple-element.171), channel_id=1, source_target_pairs={{0,1},{1,2},{2,3},{4,5},{5,6},{6,7},{8,9},{9,10},{10,11},{12,13},{... | collective-permute-start | bytes 36872 | tf_op jit(solution)/shard_map/ppermute | solution.py:20
  209.1 14.2 %collective-permute-start.4 = (f32[3,1,16,512]{3,2,1,0:T(8,128)}, f32[3,1,16,512]{3,2,1,0:T(8,128)}, u32[]{:S(2)}, u32[]{:S(2)}) collective-permute-start(f32[3,1,16,512]{3,2,1,0:T(8,128)} %get-tuple-element.165), channel_id=1, source_target_pairs={{4,0},{8,4},{12,8},{16,12},{20,16},{24,20},{28,24},{32,28},{36,32}... | collective-permute-start | bytes 294920 | tf_op jit(solution)/shard_map/ppermute | solution.py:21
  211.0 12.2 %collective-permute-start.5 = (f32[3,1,16,512]{3,2,1,0:T(8,128)}, f32[3,1,16,512]{3,2,1,0:T(8,128)}, u32[]{:S(2)}, u32[]{:S(2)}) collective-permute-start(f32[3,1,16,512]{3,2,1,0:T(8,128)} %get-tuple-element.164), channel_id=1, source_target_pairs={{0,4},{4,8},{8,12},{12,16},{16,20},{20,24},{24,28},{28,32},{32,36}... | collective-permute-start | bytes 294920 | tf_op jit(solution)/shard_map/ppermute | solution.py:20
  213.4 9.8 %collective-permute-start.6 = (f32[3,2,1,512]{3,2,1,0:T(1,128)}, f32[3,2,1,512]{3,2,1,0:T(1,128)}, u32[]{:S(2)}, u32[]{:S(2)}) collective-permute-start(f32[3,2,1,512]{3,2,1,0:T(1,128)} %get-tuple-element.163), channel_id=1, source_target_pairs={{1,0},{2,1},{3,2},{5,4},{6,5},{7,6},{9,8},{10,9},{11,10},{13,12},{... | collective-permute-start | bytes 36872 | tf_op jit(solution)/shard_map/ppermute | solution.py:21
  215.9 7.3 collective-permute-start.7
  400.1 14.2 %collective-permute-start.8 = (f32[3,1,16,512]{3,2,1,0:T(8,128)}, f32[3,1,16,512]{3,2,1,0:T(8,128)}, u32[]{:S(2)}, u32[]{:S(2)}) collective-permute-start(f32[3,1,16,512]{3,2,1,0:T(8,128)} %get-tuple-element.155), channel_id=1, source_target_pairs={{4,0},{8,4},{12,8},{16,12},{20,16},{24,20},{28,24},{32,28},{36,32}... | collective-permute-start | bytes 294920 | tf_op jit(solution)/shard_map/ppermute | solution.py:21
  402.0 12.2 %collective-permute-start.9 = (f32[3,1,16,512]{3,2,1,0:T(8,128)}, f32[3,1,16,512]{3,2,1,0:T(8,128)}, u32[]{:S(2)}, u32[]{:S(2)}) collective-permute-start(f32[3,1,16,512]{3,2,1,0:T(8,128)} %get-tuple-element.154), channel_id=1, source_target_pairs={{0,4},{4,8},{8,12},{12,16},{16,20},{20,24},{24,28},{28,32},{32,36}... | collective-permute-start | bytes 294920 | tf_op jit(solution)/shard_map/ppermute | solution.py:20
  404.4 9.8 %collective-permute-start.10 = (f32[3,2,1,512]{3,2,1,0:T(1,128)}, f32[3,2,1,512]{3,2,1,0:T(1,128)}, u32[]{:S(2)}, u32[]{:S(2)}) collective-permute-start(f32[3,2,1,512]{3,2,1,0:T(1,128)} %get-tuple-element.153), channel_id=1, source_target_pairs={{1,0},{2,1},{3,2},{5,4},{6,5},{7,6},{9,8},{10,9},{11,10},{13,12},{... | collective-permute-start | bytes 36872 | tf_op jit(solution)/shard_map/ppermute | solution.py:21
  531.7 14.3 %collective-permute-start.12 = (f32[3,1,16,512]{3,2,1,0:T(8,128)}, f32[3,1,16,512]{3,2,1,0:T(8,128)}, u32[]{:S(2)}, u32[]{:S(2)}) collective-permute-start(f32[3,1,16,512]{3,2,1,0:T(8,128)} %get-tuple-element.145), channel_id=1, source_target_pairs={{4,0},{8,4},{12,8},{16,12},{20,16},{24,20},{28,24},{32,28},{36,32}... | collective-permute-start | bytes 294920 | tf_op jit(solution)/shard_map/ppermute | solution.py:21
  533.6 12.4 %collective-permute-start.13 = (f32[3,1,16,512]{3,2,1,0:T(8,128)}, f32[3,1,16,512]{3,2,1,0:T(8,128)}, u32[]{:S(2)}, u32[]{:S(2)}) collective-permute-start(f32[3,1,16,512]{3,2,1,0:T(8,128)} %get-tuple-element.144), channel_id=1, source_target_pairs={{0,4},{4,8},{8,12},{12,16},{16,20},{20,24},{24,28},{28,32},{32,36}... | collective-permute-start | bytes 294920 | tf_op jit(solution)/shard_map/ppermute | solution.py:20
  536.1 10.0 %collective-permute-start.14 = (f32[3,2,1,512]{3,2,1,0:T(1,128)}, f32[3,2,1,512]{3,2,1,0:T(1,128)}, u32[]{:S(2)}, u32[]{:S(2)}) collective-permute-start(f32[3,2,1,512]{3,2,1,0:T(1,128)} %get-tuple-element.143), channel_id=1, source_target_pairs={{1,0},{2,1},{3,2},{5,4},{6,5},{7,6},{9,8},{10,9},{11,10},{13,12},{... | collective-permute-start | bytes 36872 | tf_op jit(solution)/shard_map/ppermute | solution.py:21
  538.6 7.5 collective-permute-start.15
  723.2 14.4 %collective-permute-start.16 = (f32[3,1,16,512]{3,2,1,0:T(8,128)}, f32[3,1,16,512]{3,2,1,0:T(8,128)}, u32[]{:S(2)}, u32[]{:S(2)}) collective-permute-start(f32[3,1,16,512]{3,2,1,0:T(8,128)} %get-tuple-element.135), channel_id=1, source_target_pairs={{4,0},{8,4},{12,8},{16,12},{20,16},{24,20},{28,24},{32,28},{36,32}... | collective-permute-start | bytes 294920 | tf_op jit(solution)/shard_map/ppermute | solution.py:21
  725.1 12.5 %collective-permute-start.17 = (f32[3,1,16,512]{3,2,1,0:T(8,128)}, f32[3,1,16,512]{3,2,1,0:T(8,128)}, u32[]{:S(2)}, u32[]{:S(2)}) collective-permute-start(f32[3,1,16,512]{3,2,1,0:T(8,128)} %get-tuple-element.134), channel_id=1, source_target_pairs={{0,4},{4,8},{8,12},{12,16},{16,20},{20,24},{24,28},{28,32},{32,36}... | collective-permute-start | bytes 294920 | tf_op jit(solution)/shard_map/ppermute | solution.py:20
  727.6 10.0 %collective-permute-start.18 = (f32[3,2,1,512]{3,2,1,0:T(1,128)}, f32[3,2,1,512]{3,2,1,0:T(1,128)}, u32[]{:S(2)}, u32[]{:S(2)}) collective-permute-start(f32[3,2,1,512]{3,2,1,0:T(1,128)} %get-tuple-element.133), channel_id=1, source_target_pairs={{1,0},{2,1},{3,2},{5,4},{6,5},{7,6},{9,8},{10,9},{11,10},{13,12},{... | collective-permute-start | bytes 36872 | tf_op jit(solution)/shard_map/ppermute | solution.py:21
  730.3 7.2 collective-permute-start.19
  853.9 14.2 %collective-permute-start.20 = (f32[3,1,16,512]{3,2,1,0:T(8,128)}, f32[3,1,16,512]{3,2,1,0:T(8,128)}, u32[]{:S(2)}, u32[]{:S(2)}) collective-permute-start(f32[3,1,16,512]{3,2,1,0:T(8,128)} %get-tuple-element.125), channel_id=1, source_target_pairs={{4,0},{8,4},{12,8},{16,12},{20,16},{24,20},{28,24},{32,28},{36,32}... | collective-permute-start | bytes 294920 | tf_op jit(solution)/shard_map/ppermute | solution.py:21
  856.2 12.0 %collective-permute-start.21 = (f32[3,1,16,512]{3,2,1,0:T(8,128)}, f32[3,1,16,512]{3,2,1,0:T(8,128)}, u32[]{:S(2)}, u32[]{:S(2)}) collective-permute-start(f32[3,1,16,512]{3,2,1,0:T(8,128)} %get-tuple-element.124), channel_id=1, source_target_pairs={{0,4},{4,8},{8,12},{12,16},{16,20},{20,24},{24,28},{28,32},{32,36}... | collective-permute-start | bytes 294920 | tf_op jit(solution)/shard_map/ppermute | solution.py:20
  858.2 9.9 %collective-permute-start.22 = (f32[3,2,1,512]{3,2,1,0:T(1,128)}, f32[3,2,1,512]{3,2,1,0:T(1,128)}, u32[]{:S(2)}, u32[]{:S(2)}) collective-permute-start(f32[3,2,1,512]{3,2,1,0:T(1,128)} %get-tuple-element.122), channel_id=1, source_target_pairs={{1,0},{2,1},{3,2},{5,4},{6,5},{7,6},{9,8},{10,9},{11,10},{13,12},{... | collective-permute-start | bytes 36872 | tf_op jit(solution)/shard_map/ppermute | solution.py:21
  860.7 7.4 collective-permute-start.23
  (14 other events, 463.7 us)
